TPU v7x, 32 devices: a whole 2x2x4 slice. The times are simulated.
32 devices in a mesh: cand: 4 (over y, core), tensor: 8 (over z, x).
Axes of the slice: x: 2, y: 2, z: 4, core: 2. Of those that a mesh axis runs over, the one named last changes fastest.
Arguments:
- states: bfloat16 [512, 3584], P('cand'), may hold values from -60 to 60
- targets: int32 [512], replicated, may hold values from 0 to 131071
- loss_mask: int32 [512], P('cand'), may hold values 0 or 1
- cand_of: int32 [4], replicated, may hold values from 0 to 3
- lambdas: float32 [4], replicated, may hold values from 0.2 to 1
- base_q: bfloat16 [3584, 4096], P('cand', 'tensor'), may hold values from -0.09375 to 0.09375
- delta_q: bfloat16 [2, 3584, 4096], P(None, 'cand', 'tensor'), may hold values from -0.046875 to 0.046875
- base_k: bfloat16 [3584, 2048], P('cand'), may hold values from -0.09375 to 0.09375
- delta_k: bfloat16 [2, 3584, 2048], P(None, 'cand'), may hold values from -0.046875 to 0.046875
- base_v: bfloat16 [3584, 2048], P('cand'), may hold values from -0.09375 to 0.09375
- delta_v: bfloat16 [2, 3584, 2048], P(None, 'cand'), may hold values from -0.046875 to 0.046875
- base_o: bfloat16 [4096, 3584], P('tensor', 'cand'), may hold values from -0.09375 to 0.09375
- delta_o: bfloat16 [2, 4096, 3584], P(None, 'tensor', 'cand'), may hold values from -0.046875 to 0.046875
- pre_gain: float32 [3584], replicated, may hold values from 0.5 to 2
- post_gain: float32 [3584], replicated, may hold values from 0.5 to 2
- final_gain: float32 [3584], replicated, may hold values from 0.5 to 2
- unembed: bfloat16 [3584, 131072], P(None, ('cand', 'tensor')), may hold values from -0.3125 to 0.3125
Outputs:
- token_loss: float32 [512], P('cand')
- cand_loss: float32 [4], replicated
All inputs are finite; a program needn't handle non-finite values. No bound on the sum of `loss_mask` on one device may be relied on, other than what follows from the above.
Results may differ from a plain program's by a relative error of at most 0.002.
Values may be sent and summed in bfloat16 or wider, within the bound.
No kernel may reach another device: no remote copies, remote signals or barrier semaphores. Data moves between devices by JAX's collectives and lax.ppermute only.
A program may use at most 128 MiB of HBM per device.

v0:
```python
import math
import jax
import jax.numpy as jnp
from jax import lax
from jax.sharding import PartitionSpec as P

KV = 8
HEAD_SIZE = 256
CANDS = 4


def root_norm(entries, scale_gain):
    mean_square = jnp.mean(entries * entries, axis=-1, keepdims=True)
    return entries * lax.rsqrt(mean_square + 1e-06) * scale_gain


def rotate_pairs(entries, length):
    half_width = entries.shape[-1] // 2
    positions = jnp.arange(length).astype(jnp.float32)
    frequency = jnp.exp(
        -math.log(10000.0) * jnp.arange(half_width).astype(jnp.float32) * 2.0 / entries.shape[-1]
    )
    angles = positions[:, None] * frequency[None, :]
    cosine = jnp.cos(angles)[:, None, :]
    sine_part = jnp.sin(angles)[:, None, :]
    first = entries[..., :half_width]
    second = entries[..., half_width:]
    return jnp.concatenate(
        [first * cosine - second * sine_part, second * cosine + first * sine_part], axis=-1
    )


def task_total(delta):
    return jnp.sum(delta.astype(jnp.float32), axis=0).astype(jnp.bfloat16)


def merge_weights(base, total, mixing):
    return (base.astype(jnp.float32) + mixing * total.astype(jnp.float32)).astype(jnp.bfloat16)


def on_device(
    states,
    targets,
    loss_mask,
    cand_of,
    lambdas,
    base_q,
    delta_q,
    base_k,
    delta_k,
    base_v,
    delta_v,
    base_o,
    delta_o,
    pre_gain,
    post_gain,
    final_gain,
    unembed,
):
    cand_id = lax.axis_index("cand")
    tensor_id = lax.axis_index("tensor")
    tensor_count = lax.axis_size("tensor")
    chosen = cand_of[cand_id]
    mixing = lambdas[chosen]
    group_size = tensor_count // KV
    head_start = tensor_id // group_size * HEAD_SIZE
    own_base_k = lax.dynamic_slice_in_dim(base_k, head_start, HEAD_SIZE, 1)
    own_base_v = lax.dynamic_slice_in_dim(base_v, head_start, HEAD_SIZE, 1)
    own_delta_k = lax.dynamic_slice_in_dim(delta_k, head_start, HEAD_SIZE, 2)
    own_delta_v = lax.dynamic_slice_in_dim(delta_v, head_start, HEAD_SIZE, 2)
    summed = [task_total(delta) for delta in (delta_q, own_delta_k, own_delta_v, delta_o)]
    pieces = (
        lax.all_gather(base_q, "cand", axis=0, tiled=True),
        lax.all_gather(own_base_k, "cand", axis=0, tiled=True),
        lax.all_gather(own_base_v, "cand", axis=0, tiled=True),
        lax.all_gather(base_o, "cand", axis=1, tiled=True),
        lax.all_gather(summed[0], "cand", axis=0, tiled=True),
        lax.all_gather(summed[1], "cand", axis=0, tiled=True),
        lax.all_gather(summed[2], "cand", axis=0, tiled=True),
        lax.all_gather(summed[3], "cand", axis=1, tiled=True),
    )
    base_parts = pieces[:4]
    task_parts = pieces[4:]
    w_query = merge_weights(base_parts[0], task_parts[0], mixing)
    w_key = merge_weights(base_parts[1], task_parts[1], mixing)
    w_value = merge_weights(base_parts[2], task_parts[2], mixing)
    w_out = merge_weights(base_parts[3], task_parts[3], mixing)
    length = states.shape[0]
    stream = states.astype(jnp.float32)
    normed = root_norm(stream, pre_gain).astype(jnp.bfloat16)
    query_rows = jnp.dot(normed, w_query, preferred_element_type=jnp.float32).reshape(
        length, -1, HEAD_SIZE
    )
    query_rows = rotate_pairs(query_rows, length).astype(jnp.bfloat16)
    key_full = jnp.dot(normed, w_key, preferred_element_type=jnp.float32).astype(jnp.bfloat16)
    value_full = jnp.dot(normed, w_value, preferred_element_type=jnp.float32).astype(jnp.bfloat16)
    key_matrix = rotate_pairs(
        key_full.astype(jnp.float32).reshape(length, 1, HEAD_SIZE), length
    ).astype(jnp.bfloat16)[:, 0, :]
    attention_scores = jnp.einsum(
        "lhd,md->hlm", query_rows, key_matrix, preferred_element_type=jnp.float32
    ) * HEAD_SIZE ** (-0.5)
    attention_scores = 50.0 * jnp.tanh(attention_scores / 50.0)
    causal = jnp.arange(length)[:, None] >= jnp.arange(length)[None, :]
    weights = jnp.where(causal[None, :, :], jnp.exp(attention_scores), 0.0)
    attention_probs = (weights / jnp.sum(weights, axis=-1, keepdims=True)).astype(jnp.bfloat16)
    context_rows = jnp.einsum(
        "hlm,md->lhd", attention_probs, value_full, preferred_element_type=jnp.float32
    )
    context_rows = context_rows.astype(jnp.bfloat16).reshape(length, -1)
    partial_value = jnp.dot(context_rows, w_out, preferred_element_type=jnp.float32)
    vocab_width = unembed.shape[1]
    vocab_start = (cand_id * tensor_count + tensor_id) * vocab_width
    vocab_index = jnp.arange(vocab_width)
    attended = lax.psum(partial_value, "tensor")
    final_rows = root_norm(stream + root_norm(attended, post_gain), final_gain).astype(jnp.bfloat16)
    logits = jnp.dot(
        lax.all_gather(final_rows, "cand", axis=0, tiled=True),
        unembed,
        preferred_element_type=jnp.float32,
    )
    capped = 30.0 * jnp.tanh(logits / 30.0)
    totals = jnp.sum(jnp.exp(capped), axis=1)
    local_ids = targets - vocab_start
    matches = local_ids[:, None] == vocab_index[None, :]
    picked = jnp.sum(jnp.where(matches, capped, 0.0), axis=1)
    vocab_sums = jnp.stack([totals, picked], axis=0)
    summed_terms = lax.psum(vocab_sums, ("cand", "tensor"))
    own_terms = lax.dynamic_slice_in_dim(summed_terms, cand_id * length, length, 1)
    mask_values = loss_mask.astype(jnp.float32)
    token_loss = mask_values * (jnp.log(own_terms[0]) - own_terms[1])
    onehot = (chosen == jnp.arange(CANDS)).astype(jnp.float32)
    loss_sums, counts = lax.psum(
        (onehot * jnp.sum(token_loss), onehot * jnp.sum(mask_values)), "cand"
    )
    return (token_loss, loss_sums / jnp.maximum(counts, 1.0))


def solution(mesh):
    in_specs = (
        P("cand", None),
        P(),
        P("cand"),
        P(),
        P(),
        P("cand", "tensor"),
        P(None, "cand", "tensor"),
        P("cand", None),
        P(None, "cand", None),
        P("cand", None),
        P(None, "cand", None),
        P("tensor", "cand"),
        P(None, "tensor", "cand"),
        P(),
        P(),
        P(),
        P(None, ("cand", "tensor")),
    )
    out_specs = (P("cand"), P())
    return jax.shard_map(
        on_device, mesh=mesh, in_specs=in_specs, out_specs=out_specs, check_vma=False
    )
```

profile of v0, /device:TPU:0, one launch (start us, length us, event | category | flops | bytes accessed | tf_op | source)
XLA Modules:
  0.0 451.5 jit_solution(439209231556427896)
XLA Ops:
  7.2 1.9 constant_dynamic-slice_fusion.1
  9.2 2.3 dynamic-slice_reduce_fusion
  11.6 1.6 reduce_sum.123
  13.2 0.5 all-gather.18.cloned.1.call-update
  13.8 1.8 constant_dynamic-slice_fusion.2
  15.7 2.4 dynamic-slice_reduce_fusion.1
  18.2 1.5 reduce_sum.125
  19.8 0.7 all-gather.22.cloned.1.call-update
  20.6 0.6 dynamic_slice.22
  23.1 0.6 dynamic_slice.23
  24.3 9.1 %all-gather.14.cloned.1.call-done = bf16[3584,256]{1,0:T(8,128)(2,1)} async-done(((bf16[896,256]{1,0:T(8,128)(2,1)}), bf16[3584,256]{1,0:T(8,128)(2,1)}) %all-gather.14.cloned.1.call-update) | async-done | bytes 1835024 | tf_op jit(solution)/shard_map/all_gather | solution.py:74
  33.4 22.7 %all-gather.16.cloned.1.call-done = bf16[3584,256]{1,0:T(8,128)(2,1)} async-done(((bf16[896,256]{1,0:T(8,128)(2,1)}), bf16[3584,256]{1,0:T(8,128)(2,1)}) %all-gather.16.cloned.1.call-update) | async-done | bytes 1835024 | tf_op jit(solution)/shard_map/all_gather | solution.py:78
  56.1 3.6 fusion.20
  60.0 29.2 %all-gather.20.cloned.1.call-done = bf16[3584,512]{1,0:T(8,128)(2,1)} async-done(((bf16[896,512]{1,0:T(8,128)(2,1)}), bf16[3584,512]{1,0:T(8,128)(2,1)}) %all-gather.20.cloned.1.call-update) | async-done | bytes 3670032 | tf_op jit(solution)/shard_map/all_gather | solution.py:77
  89.2 32.9 %all-gather.18.cloned.1.call-done = bf16[3584,512]{1,0:T(8,128)(2,1)} async-done(((bf16[896,512]{1,0:T(8,128)(2,1)}), bf16[3584,512]{1,0:T(8,128)(2,1)}) %all-gather.18.cloned.1.call-update) | async-done | bytes 3670032 | tf_op jit(solution)/shard_map/all_gather | solution.py:73
  122.1 5.2 %fusion = f32[128,512]{1,0:T(8,128)S(1)} fusion(bf16[3584,512]{1,0:T(8,128)(2,1)} %all-gather.20.cloned.1.call-done, bf16[3584,512]{1,0:T(8,128)(2,1)} %all-gather.18.cloned.1.call-done, f32[]{:T(128)} %bitcast.1, bf16[128,3584]{1,0:T(8,128)(2,1)S(1)} %copy-done.1, f32[3584]{0:T(1024)S(1)} %copy-done.8, f32[128]{0:T(128)S(1)} %add_rsqrt_fusion.2), kind=kOutput, calls=%fused_computation.6 | convolution fusion | flops 480772096 | bytes 8534532 | tf_op jit(solution)/shard_map/dot_general | solution.py:91
  127.9 16.7 %all-gather.10.cloned.1.call-done = bf16[3584,256]{1,0:T(8,128)(2,1)} async-done(((bf16[896,256]{1,0:T(8,128)(2,1)}), bf16[3584,256]{1,0:T(8,128)(2,1)}) %all-gather.10.cloned.1.call-update) | async-done | bytes 1835024 | tf_op jit(solution)/shard_map/all_gather | solution.py:75
  144.6 22.5 %all-gather.12.cloned.1.call-done = bf16[3584,256]{1,0:T(8,128)(2,1)} async-done(((bf16[896,256]{1,0:T(8,128)(2,1)}), bf16[3584,256]{1,0:T(8,128)(2,1)}) %all-gather.12.cloned.1.call-update) | async-done | bytes 1835024 | tf_op jit(solution)/shard_map/all_gather | solution.py:79
  167.2 3.9 convolution_convert_fusion
  171.1 29.1 %all-gather.24.cloned.1.call-done = bf16[512,3584]{1,0:T(8,128)(2,1)} async-done(((bf16[512,896]{1,0:T(8,128)(2,1)}), bf16[512,3584]{1,0:T(8,128)(2,1)}) %all-gather.24.cloned.1.call-update) | async-done | bytes 3670032 | tf_op jit(solution)/shard_map/all_gather | solution.py:80
  200.2 33.1 %all-gather.22.cloned.1.call-done = bf16[512,3584]{1,0:T(8,128)(2,1)} async-done(((bf16[512,896]{1,0:T(8,128)(2,1)}), bf16[512,3584]{1,0:T(8,128)(2,1)}) %all-gather.22.cloned.1.call-update) | async-done | bytes 3670032 | tf_op jit(solution)/shard_map/all_gather | solution.py:76
  233.3 6.6 %fusion.1 = f32[128,3584]{1,0:T(8,128)} fusion(bf16[128,512]{0,1:T(8,128)(2,1)S(1)} %bitcast.38, bf16[512,3584]{1,0:T(8,128)(2,1)} %all-gather.24.cloned.1.call-done, bf16[512,3584]{1,0:T(8,128)(2,1)} %all-gather.22.cloned.1.call-done, f32[]{:T(128)} %bitcast.1), kind=kOutput, calls=%fused_computation.7 | convolution fusion | flops 478937088 | bytes 9306116 | tf_op jit(solution)/shard_map/dot_general | solution.py:111
  240.2 95.7 %all-reduce.3.cloned.1.call-done = f32[128,3584]{1,0:T(8,128)} async-done(((f32[128,3584]{1,0:T(8,128)}), f32[128,3584]{1,0:T(8,128)}) %all-reduce.3.cloned.1.call-update) | async-done | bytes 1835024 | tf_op jit(solution)/shard_map/psum | solution.py:115
  335.9 1.8 multiply_reduce_fusion.1
  337.8 2.0 multiply_reduce_fusion
  339.8 1.4 multiply_convert_fusion
  341.3 31.1 %all-gather.26.cloned.1.call-done = bf16[512,3584]{1,0:T(8,128)(2,1)} async-done(((bf16[128,3584]{1,0:T(8,128)(2,1)}), bf16[512,3584]{1,0:T(8,128)(2,1)}) %all-gather.26.cloned.1.call-update) | async-done | bytes 3670032 | tf_op jit(solution)/shard_map/all_gather | solution.py:118
  372.4 22.9 %exponential_reduce_fusion = (f32[512]{0:T(512)S(1)}, f32[512]{0:T(512)S(1)}) fusion(s32[512]{0:T(512)S(1)} %broadcast_subtract_fusion, bf16[512,3584]{1,0:T(8,128)(2,1)} %all-gather.26.cloned.1.call-done, bf16[3584,4096]{1,0:T(8,128)(2,1)} %param.33), kind=kOutput, calls=%fused_computation.2 | convolution fusion | flops 15044968448 | bytes 33036288 | tf_op jit(solution)/shard_map/dot_general | solution.py:117
  395.3 39.3 %psum.29 = f32[2,512]{1,0:T(2,128)S(1)} all-reduce(f32[2,512]{1,0:T(2,128)S(1)} %pad_maximum_fusion), channel_id=1, replica_groups=mesh['cand'=4,'tensor'=8] {'cand','tensor'}, use_global_device_ids=true, to_apply=%region_11.12 | all-reduce | flops 1024 | bytes 8192 | tf_op jit(solution)/shard_map/psum | solution.py:128
  434.7 1.1 fusion.52
  435.8 1.8 compare_select_fusion
  437.6 6.5 %all-reduce = (f32[4]{0:T(128)S(1)}, f32[4]{0:T(128)S(1)}) all-reduce(f32[4]{0:T(128)S(1)} %get-tuple-element.18, f32[4]{0:T(128)S(1)} %get-tuple-element.17), channel_id=1, replica_groups=mesh['cand'=4,'tensor'=8] {'cand'}, use_global_device_ids=true, to_apply=%region_13.14 | all-reduce | flops 8 | bytes 64 | tf_op jit(solution)/shard_map/psum | solution.py:133
  (57 shorter events, 2.8 us)
Async XLA Ops:
  7.2 4.4 copy-start.2
  7.2 26.2 %all-gather.14.cloned.1.call-start = ((), (), s32[]{:S(2)}) async-start(), calls=%async_computation.2 | async-start | bytes 2293760 | tf_op jit(solution)/shard_map/all_gather | solution.py:74
  9.2 46.9 %all-gather.16.cloned.1.call-start = ((), (), s32[]{:S(2)}) async-start(), calls=%async_computation.3 | async-start | bytes 2293760 | tf_op jit(solution)/shard_map/all_gather | solution.py:78
  11.6 77.6 %all-gather.20.cloned.1.call-start = ((), (), s32[]{:S(2)}) async-start(), calls=%async_computation.5 | async-start | bytes 4587520 | tf_op jit(solution)/shard_map/all_gather | solution.py:77
  13.2 5.0 %copy-start.3 = (bf16[2,512,896]{2,1,0:T(8,128)(2,1)S(1)}, bf16[2,512,896]{2,1,0:T(8,128)(2,1)}, u32[]{:S(2)}) copy-start(bf16[2,512,896]{2,1,0:T(8,128)(2,1)} %param.29) | copy-start | bytes 5505028
  13.2 108.9 %all-gather.18.cloned.1.call-start = ((), (), s32[]{:S(2)}) async-start(), calls=%async_computation.4 | async-start | bytes 4587520 | tf_op jit(solution)/shard_map/all_gather | solution.py:73
  13.8 130.9 %all-gather.10.cloned.1.call-start = ((), (), s32[]{:S(2)}) async-start(), calls=%async_computation | async-start | bytes 2293760 | tf_op jit(solution)/shard_map/all_gather | solution.py:75
  15.6 4.9 %copy-start.9 = (s32[4]{0:T(128)S(1)}, s32[4]{0:T(128)}, u32[]{:S(2)}) copy-start(s32[4]{0:T(128)} %param.20) | copy-start | bytes 52
  15.6 7.4 %copy-start.10 = (f32[4]{0:T(128)S(1)}, f32[4]{0:T(128)}, u32[]{:S(2)}) copy-start(f32[4]{0:T(128)} %param.21) | copy-start | bytes 52
  15.7 8.1 %copy-start.1 = (bf16[128,3584]{1,0:T(8,128)(2,1)S(1)}, bf16[128,3584]{1,0:T(8,128)(2,1)}, u32[]{:S(2)}) copy-start(bf16[128,3584]{1,0:T(8,128)(2,1)} %param.17) | copy-start | bytes 2752516
  15.7 40.4 %copy-start.8 = (f32[3584]{0:T(1024)S(1)}, f32[3584]{0:T(1024)}, u32[]{:S(2)}) copy-start(f32[3584]{0:T(1024)} %param.30) | copy-start | bytes 43012
  15.7 151.5 %all-gather.12.cloned.1.call-start = ((), (), s32[]{:S(2)}) async-start(), calls=%async_computation.1 | async-start | bytes 2293760 | tf_op jit(solution)/shard_map/all_gather | solution.py:79
  18.2 182.1 %all-gather.24.cloned.1.call-start = ((), (), s32[]{:S(2)}) async-start(), calls=%async_computation.7 | async-start | bytes 4587520 | tf_op jit(solution)/shard_map/all_gather | solution.py:80
  19.7 213.6 %all-gather.22.cloned.1.call-start = ((), (), s32[]{:S(2)}) async-start(), calls=%async_computation.6 | async-start | bytes 4587520 | tf_op jit(solution)/shard_map/all_gather | solution.py:76
  20.5 315.4 %all-reduce.3.cloned.1.call-start = ((), (), s32[]{:S(2)}) async-start(), calls=%async_computation.8 | async-start | bytes 3670016 | tf_op jit(solution)/shard_map/psum | solution.py:115
  239.9 97.8 %copy-start.4 = (f32[3584]{0:T(1024)S(1)}, f32[3584]{0:T(1024)}, u32[]{:S(2)}) copy-start(f32[3584]{0:T(1024)} %param.31) | copy-start | bytes 43012
  239.9 99.9 %copy-start.5 = (f32[3584]{0:T(1024)S(1)}, f32[3584]{0:T(1024)}, u32[]{:S(2)}) copy-start(f32[3584]{0:T(1024)} %param.32) | copy-start | bytes 43012
  239.9 132.5 %all-gather.26.cloned.1.call-start = ((), (), s32[]{:S(2)}) async-start(), calls=%async_computation.9 | async-start | bytes 4587520 | tf_op jit(solution)/shard_map/all_gather | solution.py:118
  335.9 3.9 copy-start
  337.8 3.5 copy-start.6
  341.3 93.4 %copy-start.7 = (s32[128]{0:T(128)S(1)}, s32[128]{0:T(128)}, u32[]{:S(2)}) copy-start(s32[128]{0:T(128)} %param.19) | copy-start | bytes 1540
Sparse Core Ops, SparseCore 0:
  9.5 23.8 all-gather.13
  35.0 21.0 all-gather.15
  57.7 31.4 all-gather.19
  90.6 31.4 all-gather.17
  123.5 21.0 all-gather.9
  146.1 21.0 all-gather.11
  168.7 31.4 all-gather.23
  201.8 31.4 all-gather.21
  240.1 95.7 all-reduce.2
  341.4 30.9 all-gather.25
where the time goes:
time: 452 us
  waiting for transfers between devices  324 us (72%)
  blocking collectives  45.9 us (10%)
  matrix products  42.5 us (9%)
  other arithmetic  17.5 us (4%)
  between operations  16.3 us (4%)
  local copies, waits for them, and re-layouts  5.26 us (1%)
    psum x1, waiting for transfers between devices, on_device(): attended = lax.psum(partial_value, 'tensor')  95.7 us
    psum x1, blocking collectives, on_device(): summed_terms = lax.psum(vocab_sums, ('cand', 'tensor'))  39.3 us
    all_gather x1, waiting for transfers between devices, on_device(): lax.all_gather(base_o, 'cand', axis=1, tiled=True)  33.1 us
    all_gather x1, waiting for transfers between devices, on_device(): lax.all_gather(base_q, 'cand', axis=0, tiled=True)  32.9 us
    all_gather x1, waiting for transfers between devices, on_device(): lax.all_gather(final_rows, 'cand', axis=0, tiled=True)  31.1 us
    all_gather x1, waiting for transfers between devices, on_device(): lax.all_gather(summed[0], 'cand', axis=0, tiled=True)  29.2 us
    all_gather x1, waiting for transfers between devices, on_device(): lax.all_gather(summed[3], 'cand', axis=1, tiled=True)  29.1 us
    dot_general x1, matrix products, on_device(): jnp.dot(lax.all_gather(final_rows, 'cand', axis=0, tiled=True), unembed,...  22.9 us
  transfers between devices with their start and end apart: 10, of which 10 were waited for; matrix products, arithmetic and copies ran while one was open for 6% of the time, Pallas kernels for 0%

commit v1 on v0

--- a/solution.py
+++ b/solution.py
@@ -112,7 +112,11 @@
     vocab_width = unembed.shape[1]
     vocab_start = (cand_id * tensor_count + tensor_id) * vocab_width
     vocab_index = jnp.arange(vocab_width)
-    attended = lax.psum(partial_value, "tensor")
+    attended = partial_value
+    for hop in (1, 2, 4):
+        attended = attended + lax.ppermute(
+            attended, "tensor", [(dev, dev ^ hop) for dev in range(8)]
+        )
     final_rows = root_norm(stream + root_norm(attended, post_gain), final_gain).astype(jnp.bfloat16)
     logits = jnp.dot(
         lax.all_gather(final_rows, "cand", axis=0, tiled=True),

time: 452 us -> 517 us (1.14)
  waiting for transfers between devices: 324 us -> 387 us
  starting transfers between devices: 0.59 us -> 5.93 us
    ppermute x0 -> x3, waiting for transfers between devices: none -> 159 us  [on_device(): lax.ppermute(attended, 'tensor', [(dev, dev ^ hop) for dev in range(8)])]
    psum x1 -> x0, waiting for transfers between devices: 95.7 us -> none  [on_device(): attended = lax.psum(partial_value, 'tensor')]
    ppermute x0 -> x3, starting transfers between devices: none -> 5.56 us  [on_device(): lax.ppermute(attended, 'tensor', [(dev, dev ^ hop) for dev in range(8)])]
  transfers between devices with their start and end apart: 10 -> 12, of which waited for: 10 -> 12; matrix products, arithmetic and copies ran while one was open for 6% -> 5% of each run, Pallas kernels for 0% -> 0%
where the time goes in v1:
time: 517 us; the launch traced here: 516 us
  waiting for transfers between devices  387 us (75%)
  blocking collectives  45.9 us (9%)
  matrix products  41.1 us (8%)
  between operations  16.1 us (3%)
  other arithmetic  14.8 us (3%)
  starting transfers between devices  5.93 us (1%)
  local copies, waits for them, and re-layouts  5.54 us (1%)
    ppermute x3, waiting for transfers between devices, on_device(): lax.ppermute(attended, 'tensor', [(dev, dev ^ hop) for dev in range(8)])  159 us
    psum x1, blocking collectives, on_device(): summed_terms = lax.psum(vocab_sums, ('cand', 'tensor'))  39.3 us
    all_gather x1, waiting for transfers between devices, on_device(): lax.all_gather(base_o, 'cand', axis=1, tiled=True)  33.1 us
    all_gather x1, waiting for transfers between devices, on_device(): lax.all_gather(base_q, 'cand', axis=0, tiled=True)  32.9 us
    all_gather x1, waiting for transfers between devices, on_device(): lax.all_gather(final_rows, 'cand', axis=0, tiled=True)  31.6 us
    all_gather x1, waiting for transfers between devices, on_device(): lax.all_gather(summed[0], 'cand', axis=0, tiled=True)  29.2 us
    all_gather x1, waiting for transfers between devices, on_device(): lax.all_gather(summed[3], 'cand', axis=1, tiled=True)  29.1 us
    dot_general x1, matrix products, on_device(): jnp.dot(lax.all_gather(final_rows, 'cand', axis=0, tiled=True), unembed,...  22.9 us
  transfers between devices with their start and end apart: 12, of which 12 were waited for; matrix products, arithmetic and copies ran while one was open for 5% of the time, Pallas kernels for 0%

profile of v1, /device:TPU:0, one launch (start us, length us, event | category | flops | bytes accessed | tf_op | source)
XLA Modules:
  0.0 516.3 jit_solution(12674367356437719448)
XLA Ops:
  7.2 1.9 constant_dynamic-slice_fusion.1
  9.2 2.3 dynamic-slice_reduce_fusion
  11.6 1.6 reduce_sum.123
  13.8 2.0 constant_dynamic-slice_fusion.2
  15.8 2.3 dynamic-slice_reduce_fusion.1
  18.2 1.5 reduce_sum.125
  19.8 0.7 all-gather.22.cloned.1.call-update
  24.4 9.0 %all-gather.14.cloned.1.call-done = bf16[3584,256]{1,0:T(8,128)(2,1)} async-done(((bf16[896,256]{1,0:T(8,128)(2,1)}), bf16[3584,256]{1,0:T(8,128)(2,1)}) %all-gather.14.cloned.1.call-update) | async-done | bytes 1835024 | tf_op jit(solution)/shard_map/all_gather | solution.py:74
  33.4 22.7 %all-gather.16.cloned.1.call-done = bf16[3584,256]{1,0:T(8,128)(2,1)} async-done(((bf16[896,256]{1,0:T(8,128)(2,1)}), bf16[3584,256]{1,0:T(8,128)(2,1)}) %all-gather.16.cloned.1.call-update) | async-done | bytes 1835024 | tf_op jit(solution)/shard_map/all_gather | solution.py:78
  56.1 3.6 fusion.20
  60.0 29.2 %all-gather.20.cloned.1.call-done = bf16[3584,512]{1,0:T(8,128)(2,1)} async-done(((bf16[896,512]{1,0:T(8,128)(2,1)}), bf16[3584,512]{1,0:T(8,128)(2,1)}) %all-gather.20.cloned.1.call-update) | async-done | bytes 3670032 | tf_op jit(solution)/shard_map/all_gather | solution.py:77
  89.2 32.9 %all-gather.18.cloned.1.call-done = bf16[3584,512]{1,0:T(8,128)(2,1)} async-done(((bf16[896,512]{1,0:T(8,128)(2,1)}), bf16[3584,512]{1,0:T(8,128)(2,1)}) %all-gather.18.cloned.1.call-update) | async-done | bytes 3670032 | tf_op jit(solution)/shard_map/all_gather | solution.py:73
  122.1 5.2 %fusion = f32[128,512]{1,0:T(8,128)S(1)} fusion(bf16[3584,512]{1,0:T(8,128)(2,1)} %all-gather.20.cloned.1.call-done, bf16[3584,512]{1,0:T(8,128)(2,1)} %all-gather.18.cloned.1.call-done, f32[]{:T(128)} %bitcast.1, bf16[128,3584]{1,0:T(8,128)(2,1)S(1)} %copy-done, f32[3584]{0:T(1024)S(1)} %copy-done.7, f32[128]{0:T(128)S(1)} %add_rsqrt_fusion.2), kind=kOutput, calls=%fused_computation.6 | convolution fusion | flops 480772096 | bytes 8534532 | tf_op jit(solution)/shard_map/dot_general | solution.py:91
  127.9 16.8 %all-gather.10.cloned.1.call-done = bf16[3584,256]{1,0:T(8,128)(2,1)} async-done(((bf16[896,256]{1,0:T(8,128)(2,1)}), bf16[3584,256]{1,0:T(8,128)(2,1)}) %all-gather.10.cloned.1.call-update) | async-done | bytes 1835024 | tf_op jit(solution)/shard_map/all_gather | solution.py:75
  144.6 22.5 %all-gather.12.cloned.1.call-done = bf16[3584,256]{1,0:T(8,128)(2,1)} async-done(((bf16[896,256]{1,0:T(8,128)(2,1)}), bf16[3584,256]{1,0:T(8,128)(2,1)}) %all-gather.12.cloned.1.call-update) | async-done | bytes 1835024 | tf_op jit(solution)/shard_map/all_gather | solution.py:79
  167.2 3.9 convolution_convert_fusion
  171.1 29.1 %all-gather.24.cloned.1.call-done = bf16[512,3584]{1,0:T(8,128)(2,1)} async-done(((bf16[512,896]{1,0:T(8,128)(2,1)}), bf16[512,3584]{1,0:T(8,128)(2,1)}) %all-gather.24.cloned.1.call-update) | async-done | bytes 3670032 | tf_op jit(solution)/shard_map/all_gather | solution.py:80
  200.2 33.1 %all-gather.22.cloned.1.call-done = bf16[512,3584]{1,0:T(8,128)(2,1)} async-done(((bf16[512,896]{1,0:T(8,128)(2,1)}), bf16[512,3584]{1,0:T(8,128)(2,1)}) %all-gather.22.cloned.1.call-update) | async-done | bytes 3670032 | tf_op jit(solution)/shard_map/all_gather | solution.py:76
  233.3 5.3 %fusion.1 = f32[128,3584]{1,0:T(8,128)S(1)} fusion(bf16[128,512]{0,1:T(8,128)(2,1)S(1)} %bitcast.38, bf16[512,3584]{1,0:T(8,128)(2,1)} %all-gather.24.cloned.1.call-done, bf16[512,3584]{1,0:T(8,128)(2,1)} %all-gather.22.cloned.1.call-done, f32[]{:T(128)} %bitcast.1), kind=kOutput, calls=%fused_computation.7 | convolution fusion | flops 478937088 | bytes 9306116 | tf_op jit(solution)/shard_map/dot_general | solution.py:111
  238.6 1.5 collective-permute-start
  240.1 40.7 %collective-permute-done = f32[128,3584]{1,0:T(8,128)S(1)} collective-permute-done((f32[128,3584]{1,0:T(8,128)S(1)}, f32[128,3584]{1,0:T(8,128)S(1)}, u32[]{:S(2)}, u32[]{:S(2)}) %collective-permute-start) | collective-permute-done | bytes 1835040 | tf_op jit(solution)/shard_map/ppermute | solution.py:117
  281.0 1.6 collective-permute-start.1
  282.6 39.8 %collective-permute-done.1 = f32[128,3584]{1,0:T(8,128)S(1)} collective-permute-done((f32[128,3584]{1,0:T(8,128)S(1)}, f32[128,3584]{1,0:T(8,128)S(1)}, u32[]{:S(2)}, u32[]{:S(2)}) %collective-permute-start.1) | collective-permute-done | bytes 1835040 | tf_op jit(solution)/shard_map/ppermute | solution.py:117
  322.6 2.5 collective-permute-start.2
  325.0 78.2 %collective-permute-done.2 = f32[128,3584]{1,0:T(8,128)S(1)} collective-permute-done((f32[128,3584]{1,0:T(8,128)S(1)}, f32[128,3584]{1,0:T(8,128)S(1)}, u32[]{:S(2)}, u32[]{:S(2)}) %collective-permute-start.2) | collective-permute-done | bytes 1835040 | tf_op jit(solution)/shard_map/ppermute | solution.py:117
  404.3 1.4 multiply_convert_fusion
  405.8 31.6 %all-gather.26.cloned.1.call-done = bf16[512,3584]{1,0:T(8,128)(2,1)} async-done(((bf16[128,3584]{1,0:T(8,128)(2,1)}), bf16[512,3584]{1,0:T(8,128)(2,1)}) %all-gather.26.cloned.1.call-update) | async-done | bytes 3670032 | tf_op jit(solution)/shard_map/all_gather | solution.py:122
  437.4 22.9 %exponential_reduce_fusion = (f32[512]{0:T(512)S(1)}, f32[512]{0:T(512)S(1)}) fusion(s32[512]{0:T(512)S(1)} %broadcast_subtract_fusion, bf16[512,3584]{1,0:T(8,128)(2,1)} %all-gather.26.cloned.1.call-done, bf16[3584,4096]{1,0:T(8,128)(2,1)} %param.33), kind=kOutput, calls=%fused_computation.2 | convolution fusion | flops 15044968448 | bytes 33036288 | tf_op jit(solution)/shard_map/dot_general | solution.py:121
  460.3 39.3 %psum.21 = f32[2,512]{1,0:T(2,128)S(1)} all-reduce(f32[2,512]{1,0:T(2,128)S(1)} %pad_maximum_fusion), channel_id=1, replica_groups=mesh['cand'=4,'tensor'=8] {'cand','tensor'}, use_global_device_ids=true, to_apply=%region_10.11 | all-reduce | flops 1024 | bytes 8192 | tf_op jit(solution)/shard_map/psum | solution.py:132
  499.6 1.2 fusion.52
  500.8 1.9 compare_select_fusion
  502.7 6.5 %all-reduce = (f32[4]{0:T(128)S(1)}, f32[4]{0:T(128)S(1)}) all-reduce(f32[4]{0:T(128)S(1)} %get-tuple-element.20, f32[4]{0:T(128)S(1)} %get-tuple-element.19), channel_id=1, replica_groups=mesh['cand'=4,'tensor'=8] {'cand'}, use_global_device_ids=true, to_apply=%region_12.13 | all-reduce | flops 8 | bytes 64 | tf_op jit(solution)/shard_map/psum | solution.py:137
  (60 shorter events, 5.6 us)
Async XLA Ops:
  7.2 4.4 copy-start.1
  7.2 26.2 %all-gather.14.cloned.1.call-start = ((), (), s32[]{:S(2)}) async-start(), calls=%async_computation.2 | async-start | bytes 2293760 | tf_op jit(solution)/shard_map/all_gather | solution.py:74
  9.2 46.9 %all-gather.16.cloned.1.call-start = ((), (), s32[]{:S(2)}) async-start(), calls=%async_computation.3 | async-start | bytes 2293760 | tf_op jit(solution)/shard_map/all_gather | solution.py:78
  11.5 77.6 %all-gather.20.cloned.1.call-start = ((), (), s32[]{:S(2)}) async-start(), calls=%async_computation.5 | async-start | bytes 4587520 | tf_op jit(solution)/shard_map/all_gather | solution.py:77
  13.2 108.9 %all-gather.18.cloned.1.call-start = ((), (), s32[]{:S(2)}) async-start(), calls=%async_computation.4 | async-start | bytes 4587520 | tf_op jit(solution)/shard_map/all_gather | solution.py:73
  13.7 4.5 copy-start.2
  13.8 130.9 %all-gather.10.cloned.1.call-start = ((), (), s32[]{:S(2)}) async-start(), calls=%async_computation | async-start | bytes 2293760 | tf_op jit(solution)/shard_map/all_gather | solution.py:75
  15.8 151.4 %all-gather.12.cloned.1.call-start = ((), (), s32[]{:S(2)}) async-start(), calls=%async_computation.1 | async-start | bytes 2293760 | tf_op jit(solution)/shard_map/all_gather | solution.py:79
  18.1 2.4 copy-start.8
  18.2 5.0 copy-start.9
  18.2 5.6 %copy-start = (bf16[128,3584]{1,0:T(8,128)(2,1)S(1)}, bf16[128,3584]{1,0:T(8,128)(2,1)}, u32[]{:S(2)}) copy-start(bf16[128,3584]{1,0:T(8,128)(2,1)} %param.17) | copy-start | bytes 2752516
  18.2 182.1 %all-gather.24.cloned.1.call-start = ((), (), s32[]{:S(2)}) async-start(), calls=%async_computation.7 | async-start | bytes 4587520 | tf_op jit(solution)/shard_map/all_gather | solution.py:80
  19.7 36.3 %copy-start.7 = (f32[3584]{0:T(1024)S(1)}, f32[3584]{0:T(1024)}, u32[]{:S(2)}) copy-start(f32[3584]{0:T(1024)} %param.30) | copy-start | bytes 43012
  19.8 213.5 %all-gather.22.cloned.1.call-start = ((), (), s32[]{:S(2)}) async-start(), calls=%async_computation.6 | async-start | bytes 4587520 | tf_op jit(solution)/shard_map/all_gather | solution.py:76
  20.5 416.8 %all-gather.26.cloned.1.call-start = ((), (), s32[]{:S(2)}) async-start(), calls=%async_computation.8 | async-start | bytes 4587520 | tf_op jit(solution)/shard_map/all_gather | solution.py:122
  238.6 42.2 %collective-permute-start = (f32[128,3584]{1,0:T(8,128)S(1)}, f32[128,3584]{1,0:T(8,128)S(1)}, u32[]{:S(2)}, u32[]{:S(2)}) collective-permute-start(f32[128,3584]{1,0:T(8,128)S(1)} %fusion.1), channel_id=1, source_target_pairs={{0,1},{1,0},{2,3},{3,2},{4,5},{5,4},{6,7},{7,6},{8,9},{9,8},{10,11... | collective-permute-start | bytes 5505032 | tf_op jit(solution)/shard_map/ppermute | solution.py:117
  281.0 41.4 %collective-permute-start.1 = (f32[128,3584]{1,0:T(8,128)S(1)}, f32[128,3584]{1,0:T(8,128)S(1)}, u32[]{:S(2)}, u32[]{:S(2)}) collective-permute-start(f32[128,3584]{1,0:T(8,128)S(1)} %add.89), channel_id=1, source_target_pairs={{0,2},{1,3},{2,0},{3,1},{4,6},{5,7},{6,4},{7,5},{8,10},{9,11},{10,... | collective-permute-start | bytes 5505032 | tf_op jit(solution)/shard_map/ppermute | solution.py:117
  322.6 81.1 %copy-start.3 = (f32[3584]{0:T(1024)S(1)}, f32[3584]{0:T(1024)}, u32[]{:S(2)}) copy-start(f32[3584]{0:T(1024)} %param.31) | copy-start | bytes 43012
  322.6 80.7 %collective-permute-start.2 = (f32[128,3584]{1,0:T(8,128)S(1)}, f32[128,3584]{1,0:T(8,128)S(1)}, u32[]{:S(2)}, u32[]{:S(2)}) collective-permute-start(f32[128,3584]{1,0:T(8,128)S(1)} %add.90), channel_id=1, source_target_pairs={{0,4},{1,5},{2,6},{3,7},{4,0},{5,1},{6,2},{7,3},{8,12},{9,13},{10,... | collective-permute-start | bytes 5505032 | tf_op jit(solution)/shard_map/ppermute | solution.py:117
  403.6 0.7 copy-start.4
  404.3 1.4 copy-start.5
  405.8 93.9 %copy-start.6 = (s32[128]{0:T(128)S(1)}, s32[128]{0:T(128)}, u32[]{:S(2)}) copy-start(s32[128]{0:T(128)} %param.19) | copy-start | bytes 1540
Sparse Core Ops, SparseCore 0:
  9.5 23.8 all-gather.13
  35.0 21.0 all-gather.15
  57.7 31.4 all-gather.19
  90.6 31.4 all-gather.17
  123.5 21.0 all-gather.9
  146.1 21.0 all-gather.11
  168.7 31.4 all-gather.23
  201.8 31.4 all-gather.21
  405.9 31.4 all-gather.25
